TPU v7x, 32 devices: a whole 2x2x4 slice. The times are simulated.
32 devices in a mesh: grp: 4 (over y, x), dom: 8 (over z, core).
Axes of the slice: x: 2, y: 2, z: 4, core: 2. Of those that a mesh axis runs over, the one named last changes fastest.
Arguments:
- node_state: float32 [4096, 6, 128], P(('grp', 'dom')), may hold values from -6 to 6
- node_dest: int32 [4096], P(('grp', 'dom')), may hold values from 0 to 7, as said below
- seg_nodes: float32 [6, 16384], P(None, ('grp', 'dom')), may hold values from -6 to 6
- seg_conn: int32 [3, 32768], P(None, ('grp', 'dom')), may hold values from 0 to 511
- pair_seg: int32 [32, 4, 32], P(('grp', 'dom')), may hold values from 0 to 7
- pair_slot: int32 [32, 4, 32], P(('grp', 'dom')), may hold values from 0 to 255, as said below
Outputs:
- node_force: float32 [4096, 3, 128], P(('grp', 'dom'))
Inputs may be any that keep to these rules, and one draw needn't show every extreme that they name: `node_dest`: at most 32 blocks of one device name the same contact domain; in every grp row one contact domain receives exactly 32 blocks from every device of that row; every device sends at least one block to the contact domain of its own dom index. `pair_slot`: every entry names a slot d * 32 + k that holds a block: device (r, d) sends more than k blocks to the contact domain.
All inputs are finite; a program needn't handle non-finite values.
Results may differ from a plain program's by a relative error of at most 0.00023.
Values sent between devices are 32-bit elements; how exact they have to be, the bound alone decides.
A program may use at most 64 MiB of HBM per device.

v0:
```python
import jax
import jax.numpy as jnp
from jax import lax
from jax.sharding import PartitionSpec as P

SEG_BLK = 128
time_step = 0.5
stiffness = 0.5
radius_sq = 0.5


def seg_geometry(corners):
    corner_a = corners[:, 0]
    corner_b = corners[:, 1]
    corner_c = corners[:, 2]
    edge_one = corner_b[0:3] - corner_a[0:3]
    edge_two = corner_c[0:3] - corner_a[0:3]
    normal = 0.5 * jnp.stack(
        [
            edge_one[1] * edge_two[2] - edge_one[2] * edge_two[1],
            edge_one[2] * edge_two[0] - edge_one[0] * edge_two[2],
            edge_one[0] * edge_two[1] - edge_one[1] * edge_two[0],
        ]
    )
    centre = (corner_a[0:3] + corner_b[0:3] + corner_c[0:3]) / 3.0
    motion = (corner_a[3:6] + corner_b[3:6] + corner_c[3:6]) / 3.0
    return jnp.concatenate([normal, centre, motion], axis=0)


def tile_force(node_rows, geometry):
    clearance = jnp.zeros((geometry.shape[1], node_rows.shape[1]), jnp.float32)
    distance = jnp.zeros((geometry.shape[1], node_rows.shape[1]), jnp.float32)
    for axis_id in range(3):
        offset = node_rows[axis_id][None, :] - geometry[3 + axis_id][:, None]
        drift = node_rows[3 + axis_id][None, :] - geometry[6 + axis_id][:, None]
        clearance = clearance + geometry[axis_id][:, None] * (offset + time_step * drift)
        distance = distance + offset * offset
    pressure = stiffness * jnp.exp(-distance / radius_sq) * jnp.maximum(-clearance, 0.0)
    return jnp.dot(
        geometry[0:3], pressure, precision=lax.Precision.HIGHEST, preferred_element_type=jnp.float32
    )


def place_rows(slot_ids, values, slot_total):
    onehot = (slot_ids[None, :] == jnp.arange(slot_total, dtype=jnp.int32)[:, None]).astype(
        jnp.float32
    )
    flattened = values.reshape(values.shape[0], -1)
    placed = jnp.dot(
        onehot, flattened, precision=lax.Precision.HIGHEST, preferred_element_type=jnp.float32
    )
    return placed.reshape((slot_total,) + values.shape[1:])


def shards(node_state, node_dest, seg_nodes, seg_conn, pair_seg, pair_slot):
    dom_count = lax.axis_size("dom")
    grp_count = lax.axis_size("grp")
    block_count = node_state.shape[0]
    capacity = max(2, 2 * block_count // dom_count)
    slot_count = dom_count * capacity
    order_ids = jnp.arange(block_count, dtype=jnp.int32)
    earlier = order_ids[None, :] < order_ids[:, None]
    same_dom = node_dest[:, None] == node_dest[None, :]
    slot_rank = jnp.sum((same_dom & earlier).astype(jnp.int32), axis=1)
    target_slot = node_dest * capacity + slot_rank
    outgoing = place_rows(target_slot, node_state, slot_count)
    received = lax.all_to_all(outgoing, "dom", split_axis=0, concat_axis=0, tiled=True)
    corners = jnp.take(seg_nodes, seg_conn, axis=1)
    geometry = seg_geometry(corners)
    seg_blocks = geometry.shape[1] // SEG_BLK
    geo_blocks = jnp.transpose(geometry.reshape(9, seg_blocks, SEG_BLK), (1, 0, 2))
    seg_table = pair_seg[0]
    slot_table = pair_slot[0]
    geo_all = lax.all_gather(geo_blocks, "grp", axis=0, tiled=True)
    seg_in, slot_in = (
        lax.all_to_all(seg_table, "grp", split_axis=0, concat_axis=0, tiled=True),
        lax.all_to_all(slot_table, "grp", split_axis=0, concat_axis=0, tiled=True),
    )
    owner_base = (jnp.arange(grp_count, dtype=jnp.int32) * seg_blocks)[:, None]
    seg_ids = (seg_in + owner_base).reshape(-1)
    slot_ids = slot_in.reshape(-1)
    forces = jax.vmap(tile_force)(
        jnp.take(received, slot_ids, axis=0), jnp.take(geo_all, seg_ids, axis=0)
    )
    own_forces = place_rows(slot_ids, forces, slot_count)
    returned = lax.all_to_all(own_forces, "dom", split_axis=0, concat_axis=0, tiled=True)
    return jnp.take(returned, target_slot, axis=0)


def solution(mesh):
    in_specs = (
        P(("grp", "dom"), None, None),
        P(("grp", "dom")),
        P(None, ("grp", "dom")),
        P(None, ("grp", "dom")),
        P(("grp", "dom"), None, None),
        P(("grp", "dom"), None, None),
    )
    out_specs = P(("grp", "dom"), None, None)
    return jax.shard_map(shards, mesh=mesh, in_specs=in_specs, out_specs=out_specs, check_vma=False)
```

profile of v0, /device:TPU:0, one launch (start us, length us, event | category | flops | bytes accessed | tf_op | source)
XLA Modules:
  0.0 130.9 jit_solution(8303364324702544644)
XLA Ops:
  0.0 5.2 %all-to-all-start.1 = ((s32[4,1,32]{2,1,0:T(1,128)}), s32[4,1,32]{2,1,0:T(1,128)S(1)}, u32[]{:S(2)}, u32[]{:S(2)}) async-start(s32[4,1,32]{2,1,0:T(1,128)} %bitcast.88), calls=%async_computation.1 | async-start | bytes 4096 | tf_op jit(solution)/shard_map/all_to_all | solution.py:76
  5.2 0.7 compare_and_fusion
  5.9 0.7 compare_select_fusion
  6.7 0.9 convert_reduce_fusion
  7.6 0.7 compare_and_fusion.3
  8.3 0.9 copy.46
  9.1 1.2 copy.49
  10.3 8.1 %gather_fusion = f32[3072,6]{1,0:T(8,128)S(1)} fusion(f32[6,512]{0,1:T(8,128)S(1)} %copy.46, s32[3072]{0:T(1024)S(1)} %broadcast_clamp_fusion), kind=kCustom, calls=%fused_computation | custom fusion | bytes 159744 | tf_op jit(solution)/shard_map/jit(_take)/gather | solution.py:68
  18.4 0.5 copy.47
  19.0 0.5 fusion.34
  19.6 9.6 %all_gather.3 = f32[32,9,128]{2,0,1:T(8,128)S(1)} all-gather(f32[8,9,128]{2,0,1:T(8,128)S(1)} %maximum_bitcast_fusion), channel_id=1, replica_groups=mesh['grp'=4,'dom'=8] {'grp'}, dimensions={0}, use_global_device_ids=true | all-gather | bytes 184320 | tf_op jit(solution)/shard_map/all_gather | solution.py:74
  29.4 1.4 %copy.50 = f32[256,6,128]{2,1,0:T(8,128)} copy(f32[256,6,128]{2,0,1:T(8,128)S(1)} %fusion.34) | data formatting | bytes 1572864 | tf_op jit(solution)/shard_map/dot_general | solution.py:49
  30.9 3.2 %all-to-all-start = ((s32[4,1,32]{2,1,0:T(1,128)}), s32[4,1,32]{2,1,0:T(1,128)S(1)}, u32[]{:S(2)}, u32[]{:S(2)}) async-start(s32[4,1,32]{2,1,0:T(1,128)} %bitcast.1), calls=%async_computation | async-start | bytes 4096 | tf_op jit(solution)/shard_map/all_to_all | solution.py:77
  34.3 0.5 broadcast.128
  34.8 0.7 reduce.10
  35.5 3.1 %all-to-all-done = s32[4,1,32]{2,1,0:T(1,128)S(1)} async-done(((s32[4,1,32]{2,1,0:T(1,128)}), s32[4,1,32]{2,1,0:T(1,128)S(1)}, u32[]{:S(2)}, u32[]{:S(2)}) %all-to-all-start) | async-done | bytes 544 | tf_op jit(solution)/shard_map/all_to_all | solution.py:77
  38.7 4.9 %all-to-all-start.2 = ((f32[256,6,128]{2,1,0:T(8,128)}), f32[256,6,128]{2,1,0:T(8,128)S(1)}, u32[]{:S(2)}, u32[]{:S(2)}) async-start(f32[256,6,128]{2,1,0:T(8,128)} %copy.50), calls=%async_computation.2 | async-start | bytes 2097152 | tf_op jit(solution)/shard_map/all_to_all | solution.py:67
  43.6 0.7 reduce.11
  44.4 0.8 gather_fusion.1
  45.2 0.6 compare_and_fusion.1
  46.0 1.0 fusion.53
  47.0 23.1 %all-to-all-done.2 = f32[256,6,128]{2,1,0:T(8,128)S(1)} async-done(((f32[256,6,128]{2,1,0:T(8,128)}), f32[256,6,128]{2,1,0:T(8,128)S(1)}, u32[]{:S(2)}, u32[]{:S(2)}) %all-to-all-start.2) | async-done | bytes 786464 | tf_op jit(solution)/shard_map/all_to_all | solution.py:67
  70.1 0.8 gather_fusion.2
  71.1 0.3 fusion.54
  71.4 0.3 copy-done
  71.8 37.2 %fusion.14 = f32[128,3,128]{2,1,0:T(4,128)S(1)} fusion(f32[128,128]{1,0:T(8,128)S(1)} %bitcast.69, f32[128,128]{1,0:T(8,128)S(1)} %bitcast.78, f32[128,128]{1,0:T(8,128)S(1)} %bitcast.70, f32[128,128]{1,0:T(8,128)S(1)} %bitcast.71, f32[128,128]{1,0:T(8,128)S(1)} %bitcast.79, f32[128,128]{1,0:T(8,128)S(1)} %bitcast.72, f32[128,128]{1,0:T(8,128)S(1)} %bitcast.73, ...), kind=kOutput, calls=%fused_computation.24 | convolution fusion | flops 134217728 | bytes 1441792 | tf_op jit(solution)/shard_map/vmap()/dot_general | solution.py:39
  109.1 0.3 fusion.37
  109.4 1.1 copy.52
  110.5 3.5 %all-to-all-start.3 = ((f32[256,3,128]{2,1,0:T(4,128)}), f32[256,3,128]{2,1,0:T(4,128)S(1)}, u32[]{:S(2)}, u32[]{:S(2)}) async-start(f32[256,3,128]{2,1,0:T(4,128)} %copy.52), calls=%async_computation.3 | async-start | bytes 1048576 | tf_op jit(solution)/shard_map/all_to_all | solution.py:86
  114.0 15.2 %all-to-all-done.3 = f32[256,3,128]{2,1,0:T(4,128)S(1)} async-done(((f32[256,3,128]{2,1,0:T(4,128)}), f32[256,3,128]{2,1,0:T(4,128)S(1)}, u32[]{:S(2)}, u32[]{:S(2)}) %all-to-all-start.3) | async-done | bytes 393248 | tf_op jit(solution)/shard_map/all_to_all | solution.py:86
  129.3 0.8 gather_fusion.3
  130.2 0.7 copy.53
  (36 shorter events, 1.6 us)
Async XLA Ops:
  0.0 30.9 %all-to-all-start.1 = ((s32[4,1,32]{2,1,0:T(1,128)}), s32[4,1,32]{2,1,0:T(1,128)S(1)}, u32[]{:S(2)}, u32[]{:S(2)}) async-start(s32[4,1,32]{2,1,0:T(1,128)} %bitcast.88), calls=%async_computation.1 | async-start | bytes 4096 | tf_op jit(solution)/shard_map/all_to_all | solution.py:76
  30.9 7.8 %all-to-all-start = ((s32[4,1,32]{2,1,0:T(1,128)}), s32[4,1,32]{2,1,0:T(1,128)S(1)}, u32[]{:S(2)}, u32[]{:S(2)}) async-start(s32[4,1,32]{2,1,0:T(1,128)} %bitcast.1), calls=%async_computation | async-start | bytes 4096 | tf_op jit(solution)/shard_map/all_to_all | solution.py:77
  38.7 31.4 %all-to-all-start.2 = ((f32[256,6,128]{2,1,0:T(8,128)}), f32[256,6,128]{2,1,0:T(8,128)S(1)}, u32[]{:S(2)}, u32[]{:S(2)}) async-start(f32[256,6,128]{2,1,0:T(8,128)} %copy.50), calls=%async_computation.2 | async-start | bytes 2097152 | tf_op jit(solution)/shard_map/all_to_all | solution.py:67
  46.0 24.9 %copy-start.3 = (pred[128]{0:T(512)(128)(4,1)S(1)}, pred[128]{0:T(512)(128)(4,1)}, u32[]{:S(2)}) copy-start(pred[128]{0:T(512)(128)(4,1)} %compare_and_fusion.1) | copy-start | bytes 388
  70.9 0.8 copy-start
  70.9 0.9 copy-start.1
  70.9 0.9 copy-start.2
  110.5 18.8 %all-to-all-start.3 = ((f32[256,3,128]{2,1,0:T(4,128)}), f32[256,3,128]{2,1,0:T(4,128)S(1)}, u32[]{:S(2)}, u32[]{:S(2)}) async-start(f32[256,3,128]{2,1,0:T(4,128)} %copy.52), calls=%async_computation.3 | async-start | bytes 1048576 | tf_op jit(solution)/shard_map/all_to_all | solution.py:86
where the time goes:
time: 132 us; the launch traced here: 131 us
  waiting for transfers between devices  41.4 us (31%)
  matrix products  38 us (29%)
  local copies, waits for them, and re-layouts  19.1 us (14%)
  starting transfers between devices  16.8 us (13%)
  blocking collectives  9.62 us (7%)
  other arithmetic  5.68 us (4%)
    dot_general x1, matrix products, tile_force(): jnp.dot(geometry[0:3], pressure, precision=lax.Precision.HIGHEST, preferr...  37.2 us
    all_to_all x1, waiting for transfers between devices, shards(): lax.all_to_all(outgoing, 'dom', split_axis=0, concat_axis=0, tiled=True)  23.1 us
    all_to_all x1, waiting for transfers between devices, shards(): lax.all_to_all(own_forces, 'dom', split_axis=0, concat_axis=0, tiled=True)  15.2 us
    all_gather x1, blocking collectives, shards(): geo_all = lax.all_gather(geo_blocks, 'grp', axis=0, tiled=True)  9.62 us
    gather x2, local copies, waits for them, and re-layouts, shards(): corners = jnp.take(seg_nodes, seg_conn, axis=1)  8.61 us
    all_to_all x1, starting transfers between devices, shards(): lax.all_to_all(seg_table, 'grp', split_axis=0, concat_axis=0, tiled=True)  5.19 us
    all_to_all x1, starting transfers between devices, shards(): lax.all_to_all(outgoing, 'dom', split_axis=0, concat_axis=0, tiled=True)  4.88 us
    all_to_all x1, starting transfers between devices, shards(): lax.all_to_all(own_forces, 'dom', split_axis=0, concat_axis=0, tiled=True)  3.49 us
  transfers between devices with their start and end apart: 4, of which 3 were waited for; matrix products, arithmetic and copies ran while one was open for 16% of the time, Pallas kernels for 0%

commit v1 on v0

--- a/solution.py
+++ b/solution.py
@@ -71,7 +71,12 @@
     geo_blocks = jnp.transpose(geometry.reshape(9, seg_blocks, SEG_BLK), (1, 0, 2))
     seg_table = pair_seg[0]
     slot_table = pair_slot[0]
-    geo_all = lax.all_gather(geo_blocks, "grp", axis=0, tiled=True)
+    ring = [geo_blocks]
+    for hop in range(3):
+        ring.append(lax.ppermute(ring[-1], "grp", [(dev, (dev + 1) % 4) for dev in range(4)]))
+    geo_all = jnp.roll(
+        jnp.concatenate(ring[::-1], axis=0), (lax.axis_index("grp") + 1) * ring[0].shape[0], axis=0
+    )
     seg_in, slot_in = (
         lax.all_to_all(seg_table, "grp", split_axis=0, concat_axis=0, tiled=True),
         lax.all_to_all(slot_table, "grp", split_axis=0, concat_axis=0, tiled=True),

time: 132 us -> 121 us (0.917)
  blocking collectives: 9.62 us -> 0 us
  starting transfers between devices: 16.8 us -> 19.4 us
  waiting for transfers between devices: 41.4 us -> 39.4 us
  local copies, waits for them, and re-layouts: 19.1 us -> 17.7 us
    all_to_all x1, waiting for transfers between devices: 23.1 us -> 12.4 us  [shards(): lax.all_to_all(outgoing, 'dom', split_axis=0, concat_axis=0, tiled=True)]
    ppermute x0 -> x3, waiting for transfers between devices: none -> 9.98 us  [shards(): lax.ppermute(ring[-1], 'grp', [(dev, (dev + 1) % 4) for dev in range(4)])]
    all_gather x1 -> x0, blocking collectives: 9.62 us -> none  [shards(): geo_all = lax.all_gather(geo_blocks, 'grp', axis=0, tiled=True)]
    ppermute x0 -> x3, starting transfers between devices: none -> 2.65 us  [shards(): lax.ppermute(ring[-1], 'grp', [(dev, (dev + 1) % 4) for dev in range(4)])]
    all_to_all x1, waiting for transfers between devices: 3.12 us -> 1.77 us  [shards(): lax.all_to_all(slot_table, 'grp', split_axis=0, concat_axis=0, tiled=True)]
    unnamed x10 -> x18, local copies, waits for them, and re-layouts: 2.42 us -> 1.09 us
  transfers between devices with their start and end apart: 4 -> 7, of which waited for: 3 -> 5; matrix products, arithmetic and copies ran while one was open for 16% -> 15% of each run, Pallas kernels for 0% -> 0%
where the time goes in v1:
time: 121 us; the launch traced here: 120 us
  waiting for transfers between devices  39.4 us (33%)
  matrix products  38.1 us (31%)
  starting transfers between devices  19.4 us (16%)
  local copies, waits for them, and re-layouts  17.7 us (15%)
  other arithmetic  5.07 us (4%)
    dot_general x1, matrix products, tile_force(): jnp.dot(geometry[0:3], pressure, precision=lax.Precision.HIGHEST, preferr...  37.2 us
    all_to_all x1, waiting for transfers between devices, shards(): lax.all_to_all(own_forces, 'dom', split_axis=0, concat_axis=0, tiled=True)  15.2 us
    all_to_all x1, waiting for transfers between devices, shards(): lax.all_to_all(outgoing, 'dom', split_axis=0, concat_axis=0, tiled=True)  12.4 us
    ppermute x3, waiting for transfers between devices, shards(): lax.ppermute(ring[-1], 'grp', [(dev, (dev + 1) % 4) for dev in range(4)])  9.98 us
    gather x2, local copies, waits for them, and re-layouts, shards(): corners = jnp.take(seg_nodes, seg_conn, axis=1)  8.59 us
    all_to_all x1, starting transfers between devices, shards(): lax.all_to_all(seg_table, 'grp', split_axis=0, concat_axis=0, tiled=True)  5.19 us
    all_to_all x1, starting transfers between devices, shards(): lax.all_to_all(outgoing, 'dom', split_axis=0, concat_axis=0, tiled=True)  4.88 us
    all_to_all x1, starting transfers between devices, shards(): lax.all_to_all(own_forces, 'dom', split_axis=0, concat_axis=0, tiled=True)  3.49 us
  transfers between devices with their start and end apart: 7, of which 5 were waited for; matrix products, arithmetic and copies ran while one was open for 15% of the time, Pallas kernels for 0%

profile of v1, /device:TPU:0, one launch (start us, length us, event | category | flops | bytes accessed | tf_op | source)
XLA Modules:
  0.0 120.0 jit_solution(6367158374907877924)
XLA Ops:
  0.0 5.2 %all-to-all-start.1 = ((s32[4,1,32]{2,1,0:T(1,128)}), s32[4,1,32]{2,1,0:T(1,128)S(1)}, u32[]{:S(2)}, u32[]{:S(2)}) async-start(s32[4,1,32]{2,1,0:T(1,128)} %bitcast.90), calls=%async_computation.1 | async-start | bytes 4096 | tf_op jit(solution)/shard_map/all_to_all | solution.py:81
  5.2 0.7 compare_and_fusion
  5.9 0.7 compare_select_fusion
  6.7 0.9 copy.50
  7.6 8.1 %gather_fusion = f32[3072,6]{1,0:T(8,128)S(1)} fusion(f32[6,512]{0,1:T(8,128)S(1)} %copy.50, s32[3072]{0:T(1024)S(1)} %broadcast_clamp_fusion), kind=kCustom, calls=%fused_computation | custom fusion | bytes 159744 | tf_op jit(solution)/shard_map/jit(_take)/gather | solution.py:68
  15.7 0.5 copy.51
  16.3 2.1 %collective-permute-start = (f32[8,9,128]{2,1,0:T(8,128)S(1)}, f32[8,9,128]{2,1,0:T(8,128)S(1)}, u32[]{:S(2)}, u32[]{:S(2)}) collective-permute-start(f32[8,9,128]{2,1,0:T(8,128)S(1)} %maximum_bitcast_fusion), channel_id=1, source_target_pairs={{0,8},{8,16},{16,24},{24,0},{1,9},{9,17},{17,25},{25,1},{2,10},{10... | collective-permute-start | bytes 110600 | tf_op jit(solution)/shard_map/ppermute | solution.py:76
  19.0 0.5 fusion.34
  19.5 3.2 %all-to-all-start = ((s32[4,1,32]{2,1,0:T(1,128)}), s32[4,1,32]{2,1,0:T(1,128)S(1)}, u32[]{:S(2)}, u32[]{:S(2)}) async-start(s32[4,1,32]{2,1,0:T(1,128)} %bitcast.1), calls=%async_computation | async-start | bytes 4096 | tf_op jit(solution)/shard_map/all_to_all | solution.py:82
  22.8 1.4 %copy.58 = f32[256,6,128]{2,1,0:T(8,128)} copy(f32[256,6,128]{2,0,1:T(8,128)S(1)} %fusion.34) | data formatting | bytes 1572864 | tf_op jit(solution)/shard_map/dot_general | solution.py:49
  24.3 0.5 broadcast.129
  24.8 0.7 reduce.10
  25.6 1.8 %all-to-all-done = s32[4,1,32]{2,1,0:T(1,128)S(1)} async-done(((s32[4,1,32]{2,1,0:T(1,128)}), s32[4,1,32]{2,1,0:T(1,128)S(1)}, u32[]{:S(2)}, u32[]{:S(2)}) %all-to-all-start) | async-done | bytes 544 | tf_op jit(solution)/shard_map/all_to_all | solution.py:82
  27.4 4.9 %all-to-all-start.2 = ((f32[256,6,128]{2,1,0:T(8,128)}), f32[256,6,128]{2,1,0:T(8,128)S(1)}, u32[]{:S(2)}, u32[]{:S(2)}) async-start(f32[256,6,128]{2,1,0:T(8,128)} %copy.58), calls=%async_computation.2 | async-start | bytes 2097152 | tf_op jit(solution)/shard_map/all_to_all | solution.py:67
  32.3 0.7 reduce.11
  33.1 0.6 compare_and_fusion.1
  33.7 0.6 collective-permute-start.1
  34.3 4.8 %collective-permute-done.1 = f32[8,9,128]{2,1,0:T(8,128)S(1)} collective-permute-done((f32[8,9,128]{2,1,0:T(8,128)S(1)}, f32[8,9,128]{2,1,0:T(8,128)S(1)}, u32[]{:S(2)}, u32[]{:S(2)}) %collective-permute-start.1) | collective-permute-done | bytes 36896 | tf_op jit(solution)/shard_map/ppermute | solution.py:76
  39.1 5.2 %collective-permute-done.2 = f32[8,9,128]{2,1,0:T(8,128)S(1)} collective-permute-done((f32[8,9,128]{2,1,0:T(8,128)S(1)}, f32[8,9,128]{2,1,0:T(8,128)S(1)}, u32[]{:S(2)}, u32[]{:S(2)}) %collective-permute-start.2) | collective-permute-done | bytes 36896 | tf_op jit(solution)/shard_map/ppermute | solution.py:76
  44.4 0.8 gather_fusion.1
  45.4 1.0 fusion.53
  46.4 12.4 %all-to-all-done.2 = f32[256,6,128]{2,1,0:T(8,128)S(1)} async-done(((f32[256,6,128]{2,1,0:T(8,128)}), f32[256,6,128]{2,1,0:T(8,128)S(1)}, u32[]{:S(2)}, u32[]{:S(2)}) %all-to-all-start.2) | async-done | bytes 786464 | tf_op jit(solution)/shard_map/all_to_all | solution.py:67
  58.8 0.8 gather_fusion.2
  59.6 0.9 broadcast_select_fusion.1
  60.5 0.3 fusion.54
  60.8 37.2 %fusion.14 = f32[128,3,128]{2,1,0:T(4,128)S(1)} fusion(f32[128,128]{1,0:T(8,128)S(1)} %bitcast.74, f32[128,128]{1,0:T(8,128)S(1)} %bitcast.83, f32[128,128]{1,0:T(8,128)S(1)} %bitcast.75, f32[128,128]{1,0:T(8,128)S(1)} %bitcast.76, f32[128,128]{1,0:T(8,128)S(1)} %bitcast.84, f32[128,128]{1,0:T(8,128)S(1)} %bitcast.77, f32[128,128]{1,0:T(8,128)S(1)} %bitcast.78, ...), kind=kOutput, calls=%fused_computation.24 | convolution fusion | flops 134217728 | bytes 1441792 | tf_op jit(solution)/shard_map/vmap()/dot_general | solution.py:39
  98.2 0.3 fusion.37
  98.5 1.1 copy.60
  99.6 3.5 %all-to-all-start.3 = ((f32[256,3,128]{2,1,0:T(4,128)}), f32[256,3,128]{2,1,0:T(4,128)S(1)}, u32[]{:S(2)}, u32[]{:S(2)}) async-start(f32[256,3,128]{2,1,0:T(4,128)} %copy.60), calls=%async_computation.3 | async-start | bytes 1048576 | tf_op jit(solution)/shard_map/all_to_all | solution.py:91
  103.1 15.2 %all-to-all-done.3 = f32[256,3,128]{2,1,0:T(4,128)S(1)} async-done(((f32[256,3,128]{2,1,0:T(4,128)}), f32[256,3,128]{2,1,0:T(4,128)S(1)}, u32[]{:S(2)}, u32[]{:S(2)}) %all-to-all-start.3) | async-done | bytes 393248 | tf_op jit(solution)/shard_map/all_to_all | solution.py:91
  118.4 0.7 gather_fusion.3
  119.3 0.7 copy.61
  (50 shorter events, 1.8 us)
Async XLA Ops:
  0.0 19.5 %all-to-all-start.1 = ((s32[4,1,32]{2,1,0:T(1,128)}), s32[4,1,32]{2,1,0:T(1,128)S(1)}, u32[]{:S(2)}, u32[]{:S(2)}) async-start(s32[4,1,32]{2,1,0:T(1,128)} %bitcast.90), calls=%async_computation.1 | async-start | bytes 4096 | tf_op jit(solution)/shard_map/all_to_all | solution.py:81
  7.5 11.1 %copy-start.4 = (s32[128]{0:T(128)S(1)}, s32[128]{0:T(128)}, u32[]{:S(2)}) copy-start(s32[128]{0:T(128)} %param.7) | copy-start | bytes 1540
  7.6 11.3 %copy-start = (f32[128,6,128]{2,0,1:T(8,128)S(1)}, f32[128,6,128]{2,0,1:T(8,128)}, u32[]{:S(2)}) copy-start(f32[128,6,128]{2,0,1:T(8,128)} %param.6) | copy-start | bytes 1179652
  16.3 17.4 %collective-permute-start = (f32[8,9,128]{2,1,0:T(8,128)S(1)}, f32[8,9,128]{2,1,0:T(8,128)S(1)}, u32[]{:S(2)}, u32[]{:S(2)}) collective-permute-start(f32[8,9,128]{2,1,0:T(8,128)S(1)} %maximum_bitcast_fusion), channel_id=1, source_target_pairs={{0,8},{8,16},{16,24},{24,0},{1,9},{9,17},{17,25},{25,1},{2,10},{10... | collective-permute-start | bytes 110600 | tf_op jit(solution)/shard_map/ppermute | solution.py:76
  19.5 7.8 %all-to-all-start = ((s32[4,1,32]{2,1,0:T(1,128)}), s32[4,1,32]{2,1,0:T(1,128)S(1)}, u32[]{:S(2)}, u32[]{:S(2)}) async-start(s32[4,1,32]{2,1,0:T(1,128)} %bitcast.1), calls=%async_computation | async-start | bytes 4096 | tf_op jit(solution)/shard_map/all_to_all | solution.py:82
  27.4 31.4 %all-to-all-start.2 = ((f32[256,6,128]{2,1,0:T(8,128)}), f32[256,6,128]{2,1,0:T(8,128)S(1)}, u32[]{:S(2)}, u32[]{:S(2)}) async-start(f32[256,6,128]{2,1,0:T(8,128)} %copy.58), calls=%async_computation.2 | async-start | bytes 2097152 | tf_op jit(solution)/shard_map/all_to_all | solution.py:67
  33.7 5.4 %collective-permute-start.1 = (f32[8,9,128]{2,1,0:T(8,128)S(1)}, f32[8,9,128]{2,1,0:T(8,128)S(1)}, u32[]{:S(2)}, u32[]{:S(2)}) collective-permute-start(f32[8,9,128]{2,1,0:T(8,128)S(1)} %collective-permute-done), channel_id=1, source_target_pairs={{0,8},{8,16},{16,24},{24,0},{1,9},{9,17},{17,25},{25,1},{2,10},{10... | collective-permute-start | bytes 110600 | tf_op jit(solution)/shard_map/ppermute | solution.py:76
  39.1 5.2 %collective-permute-start.2 = (f32[8,9,128]{2,1,0:T(8,128)S(1)}, f32[8,9,128]{2,1,0:T(8,128)S(1)}, u32[]{:S(2)}, u32[]{:S(2)}) collective-permute-start(f32[8,9,128]{2,1,0:T(8,128)S(1)} %collective-permute-done.1), channel_id=1, source_target_pairs={{0,8},{8,16},{16,24},{24,0},{1,9},{9,17},{17,25},{25,1},{2,10},{10... | collective-permute-start | bytes 110600 | tf_op jit(solution)/shard_map/ppermute | solution.py:76
  59.6 1.2 %copy-start.1 = (f32[128,1,128]{2,1,0:T(1,128)S(1)}, f32[128,1,128]{2,1,0:T(1,128)}, u32[]{:S(2)}) copy-start(f32[128,1,128]{2,1,0:T(1,128)} %get-tuple-element.13) | copy-start | bytes 196612
  59.6 1.2 %copy-start.2 = (f32[128,1,128]{2,1,0:T(1,128)S(1)}, f32[128,1,128]{2,1,0:T(1,128)}, u32[]{:S(2)}) copy-start(f32[128,1,128]{2,1,0:T(1,128)} %get-tuple-element.14) | copy-start | bytes 196612
  59.6 1.2 %copy-start.3 = (f32[128,1,128]{2,1,0:T(1,128)S(1)}, f32[128,1,128]{2,1,0:T(1,128)}, u32[]{:S(2)}) copy-start(f32[128,1,128]{2,1,0:T(1,128)} %get-tuple-element.15) | copy-start | bytes 196612
  99.6 18.8 %all-to-all-start.3 = ((f32[256,3,128]{2,1,0:T(4,128)}), f32[256,3,128]{2,1,0:T(4,128)S(1)}, u32[]{:S(2)}, u32[]{:S(2)}) async-start(f32[256,3,128]{2,1,0:T(4,128)} %copy.60), calls=%async_computation.3 | async-start | bytes 1048576 | tf_op jit(solution)/shard_map/all_to_all | solution.py:91
